TPU v7x, 128 devices: a whole 4x4x4 slice. The times are simulated.
128 devices in a mesh: beam: 16 (over z_lo, y, core), hid: 8 (over x, z_hi).
Axes of the slice: x: 4, y: 4, z: 4 (z_hi: 2, z_lo: 2; z = z_hi * 2 + z_lo), core: 2. Of those that a mesh axis runs over, the one named last changes fastest.
Arguments:
- queries: bfloat16 [1024, 256], P('beam'), may hold values from -6 to 6
- beam_ids: int32 [1024, 256], P('beam'), may hold values from 0 to 262143, as said below
- child_table: bfloat16 [524288, 256], P('beam'), may hold values from -6 to 6
- w_query: bfloat16 [256, 1024], P(None, 'hid'), may hold values from -0.21875 to 0.21875
- w_child: bfloat16 [256, 1024], P(None, 'hid'), may hold values from -0.21875 to 0.21875
- w_cross: bfloat16 [256, 1024], P(None, 'hid'), may hold values from -0.21875 to 0.21875
- bias: float32 [1024], P('hid'), may hold values from -3 to 3
- w_out: float32 [1024], P('hid'), may hold values from -0.1875 to 0.1875
Outputs:
- scores: float32 [1024, 512], P('beam', 'hid')
Inputs may be any that keep to these rules, and one draw needn't show every extreme that they name: `beam_ids`: each id b names a node of the current level; its children are rows 2 b and 2 b + 1 of child_table. Among the ids of one index of beam's 64 queries, at most 1536 lie in the rows held by one index of beam (ids r * 16384 to (r + 1) * 16384 - 1 for index r), and in every draw one such index receives exactly 1536 from every index of beam.
All inputs are finite; a program needn't handle non-finite values.
Results may differ from a plain program's by a relative error of at most 0.0019.
Values may be sent and summed in bfloat16 or wider, within the bound.
A program may use at most 128 MiB of HBM per device.

v0:
```python
import math
import jax
import jax.numpy as jnp
from jax import lax
from jax.sharding import PartitionSpec as P


def cut_along(shard, dim, size):
    before, after = (shard.shape[:dim], shard.shape[dim + 1 :])
    return jnp.moveaxis(shard.reshape(*before, size, -1, *after), dim, 0)


def edges_of(length, count):
    hop = length // count
    if hop >= 8:
        hop -= hop % 8
    return [hop * k for k in range(1, count)]


def in_order(pieces, dim):
    pieces = jnp.moveaxis(pieces, 0, dim)
    lengths = pieces.shape
    return pieces.reshape(*lengths[:dim], lengths[dim] * lengths[dim + 1], *lengths[dim + 2 :])


def cut_exchange(shard, axis, pieces, split_dim, concat_dim):
    blocks = cut_along(shard, split_dim, lax.axis_size(axis))
    cut = max(range(1, max(2, blocks.ndim - 1)), key=lambda d: blocks.shape[d])
    gathered = []
    for share in jnp.split(blocks, edges_of(blocks.shape[cut], pieces), axis=cut):
        if share.size:
            gathered.append(lax.all_to_all(share, axis, split_axis=0, concat_axis=0, tiled=True))
    return in_order(jnp.concatenate(gathered, axis=cut), concat_dim)


def sum_at_owner(shard, axis, dim):
    size = lax.axis_size(axis)
    pieces = lax.all_to_all(cut_along(shard, dim, size), axis, 0, 0, tiled=True)
    return jnp.sum(pieces, axis=0)


def owner_ranks(owners, nbeam):
    slots = owners.shape[0]
    block = math.gcd(slots, 512)
    blocks = slots // block
    onehot = (owners[:, None] == jnp.arange(nbeam, dtype=jnp.int32)[None, :]).astype(jnp.bfloat16)
    blocked = onehot.reshape(blocks, block, nbeam)
    lower = (jnp.arange(block)[:, None] > jnp.arange(block)[None, :]).astype(jnp.bfloat16)
    inside = jnp.einsum("ij,bjn->bin", lower, blocked, preferred_element_type=jnp.float32)
    totals = jnp.sum(blocked.astype(jnp.float32), axis=1)
    before = jnp.cumsum(totals, axis=0) - totals
    counts = (inside + before[:, None, :]).reshape(slots, nbeam)
    return jnp.sum(counts * onehot.astype(jnp.float32), axis=1).astype(jnp.int32)


def place_tables(position, offsets, nbeam, capacity):
    slots = position.shape[0]
    index = jnp.arange(slots, dtype=jnp.int32)

    def per_owner(owner):
        wanted = owner * capacity + jnp.arange(capacity, dtype=jnp.int32)
        equal = wanted[:, None] == position[None, :]
        asked = jnp.sum(jnp.where(equal, offsets[None, :], 0), axis=1)
        slot_of = jnp.sum(jnp.where(equal, index[None, :], 0), axis=1)
        live = jnp.any(equal, axis=1).astype(jnp.float32)
        return (asked, slot_of, live)

    return lax.map(per_owner, jnp.arange(nbeam, dtype=jnp.int32))


def shards(queries, beam_ids, child_table, w_query, w_child, w_cross, bias, w_out):
    nbeam = lax.axis_size("beam")
    nhid = lax.axis_size("hid")
    qcount, width = beam_ids.shape
    embed = queries.shape[1]
    slots = qcount * width
    half = child_table.shape[0] // 2
    capacity = 3 * slots // (2 * nbeam)
    pairs_table = child_table.reshape(half, 2 * embed)
    flat_ids = beam_ids.reshape(slots)
    owners = flat_ids // half
    offsets = flat_ids - owners * half
    ranks = owner_ranks(owners, nbeam)
    position = owners * capacity + ranks
    requests, slot_table, live_table = place_tables(position, offsets, nbeam, capacity)
    share = capacity // nhid
    mine = lax.dynamic_slice_in_dim(requests, lax.axis_index("hid") * share, share, 1)
    found = pairs_table[lax.all_to_all(mine, "beam", split_axis=0, concat_axis=0, tiled=True)]
    gotten = cut_exchange(found, "beam", 2, 0, 0)
    fetched = lax.all_gather(gotten, "hid", axis=1, tiled=True)
    received = fetched.reshape(nbeam * capacity, 2 * embed)
    qproj = jnp.dot(queries, w_query, preferred_element_type=jnp.float32) + bias
    block = math.gcd(qcount, max(1, 1024 // width))
    blocks = qcount // block

    def score_block(packed):
        where_rows, qblock, pblock = packed
        rows = received[where_rows].reshape(block, 2 * width, embed)
        cross = (qblock[:, None, :].astype(jnp.float32) * rows.astype(jnp.float32)).astype(
            jnp.bfloat16
        )
        flat_rows = rows.reshape(block * 2 * width, embed)
        flat_cross = cross.reshape(block * 2 * width, embed)
        pre = jnp.dot(flat_rows, w_child, preferred_element_type=jnp.float32) + jnp.dot(
            flat_cross, w_cross, preferred_element_type=jnp.float32
        )
        pre = pre.reshape(block, 2 * width, -1) + pblock[:, None, :]
        return jnp.sum(jnp.maximum(pre, 0.0) * w_out, axis=-1)

    partial_scores = lax.map(
        score_block,
        (
            position.reshape(blocks, block * width),
            queries.reshape(blocks, block, embed),
            qproj.reshape(blocks, block, -1),
        ),
    )
    partial_scores = partial_scores.reshape(qcount, 2 * width)
    return sum_at_owner(partial_scores, "hid", 1)


def solution(mesh):
    return jax.shard_map(
        shards,
        mesh=mesh,
        in_specs=(
            P("beam", None),
            P("beam", None),
            P("beam", None),
            P(None, "hid"),
            P(None, "hid"),
            P(None, "hid"),
            P("hid"),
            P("hid"),
        ),
        out_specs=P("beam", "hid"),
        check_vma=False,
    )
```

profile of v0, /device:TPU:0, one launch (start us, length us, event | category | flops | bytes accessed | tf_op | source)
XLA Modules:
  0.0 969.3 jit_solution(9309029163396406707)
XLA Ops:
  9.3 267.1 %while.20 = (s32[]{:T(128)}, s32[16,1536]{1,0:T(8,128)S(1)}, s32[16]{0:T(128)S(1)}, s32[16384]{0:T(1024)S(1)}, s32[16384]{0:T(1024)S(1)}, /*index=5*/s32[]{:T(128)}, s32[1]{0:T(128)}, s32[]{:T(128)}) while((s32[]{:T(128)}, s32[16,1536]{1,0:T(8,128)S(1)}, s32[16]{0:T(128)S(1)}, s32[16384]{0:T(1024)S(1)}, s32[16384]{0:T(1024)S(1)}, ...), condition=%wide.region_5.6_spmd, body=%wide.region_3.5_spmd.sunk | while | flops 75497472 | bytes 174205 | solution.py:68
  10.7 15.1 %select_reduce_fusion.2 = s32[1536]{0:T(1024)S(1)} fusion(s32[16384]{0:T(1024)S(1)} %get-tuple-element.266, s32[16384]{0:T(1024)S(1)} %get-tuple-element.265, s32[1536]{0:T(1024)S(1)} %iota_add_fusion.2), kind=kLoop, calls=%fused_computation.2.clone.1 | loop fusion | flops 75495936 | bytes 143360 | tf_op jit(solution)/shard_map/while/body/eval_jaxpr/reduce_sum | solution.py:63
  283.2 24.5 %reshape.188 = bf16[16384,512]{1,0:T(8,128)(2,1)} reshape(bf16[32768,256]{1,0:T(8,128)(2,1)} %param.14) | data formatting | bytes 33554432 | tf_op jit(solution)/shard_map/reshape | solution.py:79
  307.9 19.1 %gather_fusion.1 = bf16[3072,512]{1,0:T(8,128)(2,1)S(1)} fusion(bf16[16384,512]{1,0:T(8,128)(2,1)} %reshape.188, s32[3072]{0:T(1024)S(1)} %broadcast_clamp_fusion.1), kind=kCustom, calls=%fused_computation.1 | custom fusion | bytes 6303744 | tf_op jit(solution)/shard_map/gather | solution.py:88
  327.2 27.6 %all_to_all.27 = bf16[16,1,96,512]{3,2,1,0:T(8,128)(2,1)S(1)} all-to-all(bf16[16,1,96,512]{3,2,1,0:T(8,128)(2,1)S(1)} %get-tuple-element.155), channel_id=1, replica_groups=mesh['beam'=16,'hid'=8] {'beam'}, dimensions={0} | all-to-all | bytes 3145728 | tf_op jit(solution)/shard_map/all_to_all | solution.py:32
  354.8 24.7 %all_to_all.28 = bf16[16,1,96,512]{3,2,1,0:T(8,128)(2,1)S(1)} all-to-all(bf16[16,1,96,512]{3,2,1,0:T(8,128)(2,1)S(1)} %get-tuple-element.154), channel_id=1, replica_groups=mesh['beam'=16,'hid'=8] {'beam'}, dimensions={0} | all-to-all | bytes 3145728 | tf_op jit(solution)/shard_map/all_to_all | solution.py:32
  383.8 259.6 %all-gather.3.cloned.1.call-done = bf16[16,1,1536,512]{3,2,1,0:T(8,128)(2,1)} async-done(((bf16[16,1,192,512]{3,2,1,0:T(8,128)(2,1)}), bf16[16,1,1536,512]{3,2,1,0:T(8,128)(2,1)}) %all-gather.3.cloned.1.call-update) | async-done | bytes 25165840 | tf_op jit(solution)/shard_map/all_gather | solution.py:90
  643.4 306.0 %while.21 = (s32[]{:T(128)}, f32[16,4,512]{2,1,0:T(4,128)S(1)}, s32[16,1024]{1,0:T(8,128)S(1)}, bf16[24576,512]{1,0:T(8,128)(2,1)}, bf16[256,128]{1,0:T(8,128)(2...) while((s32[]{:T(128)}, f32[16,4,512]{2,1,0:T(4,128)S(1)}, ...), condition=%wide.region_8.9_spmd, body=%wide.region_6.8_spmd.sunk | while | flops 271322112 | bytes 14893693 | solution.py:110
  644.8 15.4 %gather_fusion = bf16[1024,512]{1,0:T(8,128)(2,1)S(1)} fusion(bf16[24576,512]{1,0:T(8,128)(2,1)} %get-tuple-element.293, s32[1024]{0:T(1024)S(1)} %broadcast_clamp_fusion.3), kind=kCustom, calls=%fused_computation.clone.1 | custom fusion | bytes 2101248 | tf_op jit(solution)/shard_map/while/body/eval_jaxpr/gather | solution.py:98
  663.9 15.4 %gather_fusion = bf16[1024,512]{1,0:T(8,128)(2,1)S(1)} fusion(bf16[24576,512]{1,0:T(8,128)(2,1)} %get-tuple-element.293, s32[1024]{0:T(1024)S(1)} %broadcast_clamp_fusion.3), kind=kCustom, calls=%fused_computation.clone.1 | custom fusion | bytes 2101248 | tf_op jit(solution)/shard_map/while/body/eval_jaxpr/gather | solution.py:98
  683.1 15.4 %gather_fusion = bf16[1024,512]{1,0:T(8,128)(2,1)S(1)} fusion(bf16[24576,512]{1,0:T(8,128)(2,1)} %get-tuple-element.293, s32[1024]{0:T(1024)S(1)} %broadcast_clamp_fusion.3), kind=kCustom, calls=%fused_computation.clone.1 | custom fusion | bytes 2101248 | tf_op jit(solution)/shard_map/while/body/eval_jaxpr/gather | solution.py:98
  702.2 15.4 %gather_fusion = bf16[1024,512]{1,0:T(8,128)(2,1)S(1)} fusion(bf16[24576,512]{1,0:T(8,128)(2,1)} %get-tuple-element.293, s32[1024]{0:T(1024)S(1)} %broadcast_clamp_fusion.3), kind=kCustom, calls=%fused_computation.clone.1 | custom fusion | bytes 2101248 | tf_op jit(solution)/shard_map/while/body/eval_jaxpr/gather | solution.py:98
  721.3 15.4 %gather_fusion = bf16[1024,512]{1,0:T(8,128)(2,1)S(1)} fusion(bf16[24576,512]{1,0:T(8,128)(2,1)} %get-tuple-element.293, s32[1024]{0:T(1024)S(1)} %broadcast_clamp_fusion.3), kind=kCustom, calls=%fused_computation.clone.1 | custom fusion | bytes 2101248 | tf_op jit(solution)/shard_map/while/body/eval_jaxpr/gather | solution.py:98
  740.5 15.4 %gather_fusion = bf16[1024,512]{1,0:T(8,128)(2,1)S(1)} fusion(bf16[24576,512]{1,0:T(8,128)(2,1)} %get-tuple-element.293, s32[1024]{0:T(1024)S(1)} %broadcast_clamp_fusion.3), kind=kCustom, calls=%fused_computation.clone.1 | custom fusion | bytes 2101248 | tf_op jit(solution)/shard_map/while/body/eval_jaxpr/gather | solution.py:98
  759.5 15.4 %gather_fusion = bf16[1024,512]{1,0:T(8,128)(2,1)S(1)} fusion(bf16[24576,512]{1,0:T(8,128)(2,1)} %get-tuple-element.293, s32[1024]{0:T(1024)S(1)} %broadcast_clamp_fusion.3), kind=kCustom, calls=%fused_computation.clone.1 | custom fusion | bytes 2101248 | tf_op jit(solution)/shard_map/while/body/eval_jaxpr/gather | solution.py:98
  778.7 15.4 %gather_fusion = bf16[1024,512]{1,0:T(8,128)(2,1)S(1)} fusion(bf16[24576,512]{1,0:T(8,128)(2,1)} %get-tuple-element.293, s32[1024]{0:T(1024)S(1)} %broadcast_clamp_fusion.3), kind=kCustom, calls=%fused_computation.clone.1 | custom fusion | bytes 2101248 | tf_op jit(solution)/shard_map/while/body/eval_jaxpr/gather | solution.py:98
  797.8 15.4 %gather_fusion = bf16[1024,512]{1,0:T(8,128)(2,1)S(1)} fusion(bf16[24576,512]{1,0:T(8,128)(2,1)} %get-tuple-element.293, s32[1024]{0:T(1024)S(1)} %broadcast_clamp_fusion.3), kind=kCustom, calls=%fused_computation.clone.1 | custom fusion | bytes 2101248 | tf_op jit(solution)/shard_map/while/body/eval_jaxpr/gather | solution.py:98
  816.9 15.4 %gather_fusion = bf16[1024,512]{1,0:T(8,128)(2,1)S(1)} fusion(bf16[24576,512]{1,0:T(8,128)(2,1)} %get-tuple-element.293, s32[1024]{0:T(1024)S(1)} %broadcast_clamp_fusion.3), kind=kCustom, calls=%fused_computation.clone.1 | custom fusion | bytes 2101248 | tf_op jit(solution)/shard_map/while/body/eval_jaxpr/gather | solution.py:98
  836.0 15.4 %gather_fusion = bf16[1024,512]{1,0:T(8,128)(2,1)S(1)} fusion(bf16[24576,512]{1,0:T(8,128)(2,1)} %get-tuple-element.293, s32[1024]{0:T(1024)S(1)} %broadcast_clamp_fusion.3), kind=kCustom, calls=%fused_computation.clone.1 | custom fusion | bytes 2101248 | tf_op jit(solution)/shard_map/while/body/eval_jaxpr/gather | solution.py:98
  855.1 15.4 %gather_fusion = bf16[1024,512]{1,0:T(8,128)(2,1)S(1)} fusion(bf16[24576,512]{1,0:T(8,128)(2,1)} %get-tuple-element.293, s32[1024]{0:T(1024)S(1)} %broadcast_clamp_fusion.3), kind=kCustom, calls=%fused_computation.clone.1 | custom fusion | bytes 2101248 | tf_op jit(solution)/shard_map/while/body/eval_jaxpr/gather | solution.py:98
  874.2 15.4 %gather_fusion = bf16[1024,512]{1,0:T(8,128)(2,1)S(1)} fusion(bf16[24576,512]{1,0:T(8,128)(2,1)} %get-tuple-element.293, s32[1024]{0:T(1024)S(1)} %broadcast_clamp_fusion.3), kind=kCustom, calls=%fused_computation.clone.1 | custom fusion | bytes 2101248 | tf_op jit(solution)/shard_map/while/body/eval_jaxpr/gather | solution.py:98
  893.4 15.4 %gather_fusion = bf16[1024,512]{1,0:T(8,128)(2,1)S(1)} fusion(bf16[24576,512]{1,0:T(8,128)(2,1)} %get-tuple-element.293, s32[1024]{0:T(1024)S(1)} %broadcast_clamp_fusion.3), kind=kCustom, calls=%fused_computation.clone.1 | custom fusion | bytes 2101248 | tf_op jit(solution)/shard_map/while/body/eval_jaxpr/gather | solution.py:98
  912.5 15.4 %gather_fusion = bf16[1024,512]{1,0:T(8,128)(2,1)S(1)} fusion(bf16[24576,512]{1,0:T(8,128)(2,1)} %get-tuple-element.293, s32[1024]{0:T(1024)S(1)} %broadcast_clamp_fusion.3), kind=kCustom, calls=%fused_computation.clone.1 | custom fusion | bytes 2101248 | tf_op jit(solution)/shard_map/while/body/eval_jaxpr/gather | solution.py:98
  931.7 15.4 %gather_fusion = bf16[1024,512]{1,0:T(8,128)(2,1)S(1)} fusion(bf16[24576,512]{1,0:T(8,128)(2,1)} %get-tuple-element.293, s32[1024]{0:T(1024)S(1)} %broadcast_clamp_fusion.3), kind=kCustom, calls=%fused_computation.clone.1 | custom fusion | bytes 2101248 | tf_op jit(solution)/shard_map/while/body/eval_jaxpr/gather | solution.py:98
  (340 shorter events, 325.8 us)
Async XLA Ops:
  6.5 376.4 %copy-start = (bf16[256,128]{1,0:T(8,128)(2,1)S(1)}, bf16[256,128]{1,0:T(8,128)(2,1)}, u32[]{:S(2)}) copy-start(bf16[256,128]{1,0:T(8,128)(2,1)} %param.15) | copy-start | bytes 196612
  277.1 30.6 %all-to-all-start = ((s32[16,1,192]{2,1,0:T(1,128)}), s32[16,1,192]{2,1,0:T(1,128)S(1)}, u32[]{:S(2)}, u32[]{:S(2)}) async-start(s32[16,1,192]{2,1,0:T(1,128)} %all_to_all.17), calls=%async_computation | async-start | bytes 32768 | tf_op jit(solution)/shard_map/all_to_all | solution.py:88
  283.2 360.2 %all-gather.3.cloned.1.call-start = ((), (), s32[]{:S(2)}) async-start(), calls=%async_computation.4 | async-start | bytes 28311552 | tf_op jit(solution)/shard_map/all_gather | solution.py:90
  381.4 0.8 copy-start.4
  381.4 0.9 copy-start.5
  381.4 1.5 copy-start.7
  381.5 262.0 %copy-start.2 = (bf16[256,128]{1,0:T(8,128)(2,1)S(1)}, bf16[256,128]{1,0:T(8,128)(2,1)}, u32[]{:S(2)}) copy-start(bf16[256,128]{1,0:T(8,128)(2,1)} %param.16) | copy-start | bytes 196612
  381.5 262.0 %copy-start.3 = (bf16[256,128]{1,0:T(8,128)(2,1)S(1)}, bf16[256,128]{1,0:T(8,128)(2,1)}, u32[]{:S(2)}) copy-start(bf16[256,128]{1,0:T(8,128)(2,1)} %param.17) | copy-start | bytes 196612
  381.5 262.0 %copy-start.6 = (f32[128]{0:T(128)S(1)}, f32[128]{0:T(128)}, u32[]{:S(2)}) copy-start(f32[128]{0:T(128)} %param.19) | copy-start | bytes 1540
  949.4 13.1 %copy-start.1 = (bf16[256,128]{1,0:T(8,128)(2,1)S(1)}, bf16[256,128]{1,0:T(8,128)(2,1)}, u32[]{:S(2)}) copy-start(bf16[256,128]{1,0:T(8,128)(2,1)} %param.15) | copy-start | bytes 196612
Sparse Core Ops, SparseCore 0:
  381.6 261.7 all-gather.2
where the time goes:
time: 972 us; the launch traced here: 969 us
  local copies, waits for them, and re-layouts  336 us (35%)
  other arithmetic  261 us (27%)
  waiting for transfers between devices  260 us (27%)
  blocking collectives  62.7 us (6%)
  matrix products  17.4 us (2%)
  between operations  13.6 us (1%)
  loops' own time  13.2 us (1%)
    all_gather x1, waiting for transfers between devices, shards(): fetched = lax.all_gather(gotten, 'hid', axis=1, tiled=True)  260 us
    gather x16, local copies, waits for them, and re-layouts, score_block(): rows = received[where_rows].reshape(block, 2 * width, embed)  246 us
    reduce_sum x16, other arithmetic, per_owner(): asked = jnp.sum(jnp.where(equal, offsets[None, :], 0), axis=1)  242 us
    all_to_all x2, blocking collectives, cut_exchange(): lax.all_to_all(share, axis, split_axis=0, concat_axis=0, tiled=True)  52.3 us
    reshape x1, local copies, waits for them, and re-layouts, shards(): pairs_table = child_table.reshape(half, 2 * embed)  24.5 us
  transfers between devices with their start and end apart: 2, of which 1 were waited for; matrix products, arithmetic and copies ran while one was open for 3% of the time, Pallas kernels for 0%

commit v1 on v0

--- a/solution.py
+++ b/solution.py
@@ -3,6 +3,12 @@
 import jax.numpy as jnp
 from jax import lax
 from jax.sharding import PartitionSpec as P
+
+
+def number_lots_all(z_in):
+    taken_in = jnp.stack([z_in for _ in range(jax.lax.axis_size("hid"))], axis=0)
+    tmp = jax.lax.all_to_all(taken_in, "hid", concat_axis=0, split_axis=0)
+    return jnp.concatenate(tmp, axis=1)
 
 
 def cut_along(shard, dim, size):
@@ -87,7 +93,7 @@
     mine = lax.dynamic_slice_in_dim(requests, lax.axis_index("hid") * share, share, 1)
     found = pairs_table[lax.all_to_all(mine, "beam", split_axis=0, concat_axis=0, tiled=True)]
     gotten = cut_exchange(found, "beam", 2, 0, 0)
-    fetched = lax.all_gather(gotten, "hid", axis=1, tiled=True)
+    fetched = number_lots_all(gotten)
     received = fetched.reshape(nbeam * capacity, 2 * embed)
     qproj = jnp.dot(queries, w_query, preferred_element_type=jnp.float32) + bias
     block = math.gcd(qcount, max(1, 1024 // width))

time: 972 us -> 1070 us (1.10)
  waiting for transfers between devices: 260 us -> 338 us
  local copies, waits for them, and re-layouts: 336 us -> 365 us
  between operations: 13.6 us -> 0.22 us
    all_to_all x0 -> x1, waiting for transfers between devices: none -> 338 us  [number_lots_all(): tmp = jax.lax.all_to_all(taken_in, 'hid', concat_axis=0, split_axis=0)]
    all_gather x1 -> x0, waiting for transfers between devices: 260 us -> none  [shards(): fetched = lax.all_gather(gotten, 'hid', axis=1, tiled=True)]
    all_to_all x0 -> x1, local copies, waits for them, and re-layouts: none -> 21 us  [number_lots_all(): tmp = jax.lax.all_to_all(taken_in, 'hid', concat_axis=0, split_axis=0)]
  transfers between devices with their start and end apart: 2 -> 2, of which waited for: 1 -> 1; matrix products, arithmetic and copies ran while one was open for 3% -> 2% of each run, Pallas kernels for 0% -> 0%
where the time goes in v1:
time: 1070 us
  local copies, waits for them, and re-layouts  365 us (34%)
  waiting for transfers between devices  338 us (32%)
  other arithmetic  259 us (24%)
  blocking collectives  64.7 us (6%)
  matrix products  17.3 us (2%)
  starting transfers between devices  13.5 us (1%)
  loops' own time  13.2 us (1%)
    all_to_all x1, waiting for transfers between devices, number_lots_all(): tmp = jax.lax.all_to_all(taken_in, 'hid', concat_axis=0, split_axis=0)  338 us
    gather x16, local copies, waits for them, and re-layouts, score_block(): rows = received[where_rows].reshape(block, 2 * width, embed)  246 us
    reduce_sum x16, other arithmetic, per_owner(): asked = jnp.sum(jnp.where(equal, offsets[None, :], 0), axis=1)  242 us
    all_to_all x2, blocking collectives, cut_exchange(): lax.all_to_all(share, axis, split_axis=0, concat_axis=0, tiled=True)  52.3 us
    reshape x1, local copies, waits for them, and re-layouts, shards(): pairs_table = child_table.reshape(half, 2 * embed)  24.5 us
  transfers between devices with their start and end apart: 2, of which 1 were waited for; matrix products, arithmetic and copies ran while one was open for 2% of the time, Pallas kernels for 0%

profile of v1, /device:TPU:0, one launch (start us, length us, event | category | flops | bytes accessed | tf_op | source)
XLA Modules:
  0.0 1070.7 jit_solution(6186964880532380224)
XLA Ops:
  2.8 267.1 %while.20 = (s32[]{:T(128)}, s32[16,1536]{1,0:T(8,128)S(1)}, s32[16]{0:T(128)S(1)}, s32[16384]{0:T(1024)S(1)}, s32[16384]{0:T(1024)S(1)}, /*index=5*/s32[]{:T(128)}, s32[1]{0:T(128)}, s32[]{:T(128)}) while((s32[]{:T(128)}, s32[16,1536]{1,0:T(8,128)S(1)}, s32[16]{0:T(128)S(1)}, s32[16384]{0:T(1024)S(1)}, s32[16384]{0:T(1024)S(1)}, ...), condition=%wide.region_5.6_spmd, body=%wide.region_3.5_spmd.sunk | while | flops 75497472 | bytes 174197 | solution.py:74
  276.7 24.5 %reshape.187 = bf16[16384,512]{1,0:T(8,128)(2,1)} reshape(bf16[32768,256]{1,0:T(8,128)(2,1)} %param.14) | data formatting | bytes 33554432 | tf_op jit(solution)/shard_map/reshape | solution.py:85
  301.3 19.1 %gather_fusion.1 = bf16[3072,512]{1,0:T(8,128)(2,1)S(1)} fusion(bf16[16384,512]{1,0:T(8,128)(2,1)} %reshape.187, s32[3072]{0:T(1024)S(1)} %broadcast_clamp_fusion.1), kind=kCustom, calls=%fused_computation.1 | custom fusion | bytes 6303744 | tf_op jit(solution)/shard_map/gather | solution.py:94
  320.6 27.6 %all_to_all.32 = bf16[16,1,96,512]{3,2,1,0:T(8,128)(2,1)S(1)} all-to-all(bf16[16,1,96,512]{3,2,1,0:T(8,128)(2,1)S(1)} %get-tuple-element.154), channel_id=1, replica_groups=mesh['beam'=16,'hid'=8] {'beam'}, dimensions={0} | all-to-all | bytes 3145728 | tf_op jit(solution)/shard_map/all_to_all | solution.py:38
  348.2 24.7 %all_to_all.33 = bf16[16,1,96,512]{3,2,1,0:T(8,128)(2,1)S(1)} all-to-all(bf16[16,1,96,512]{3,2,1,0:T(8,128)(2,1)S(1)} %get-tuple-element.155), channel_id=1, replica_groups=mesh['beam'=16,'hid'=8] {'beam'}, dimensions={0} | all-to-all | bytes 3145728 | tf_op jit(solution)/shard_map/all_to_all | solution.py:38
  390.8 338.2 %all-to-all-done.3 = bf16[8,16,192,512]{3,2,1,0:T(8,128)(2,1)} async-done(((bf16[8,16,192,512]{3,2,1,0:T(8,128)(2,1)}), bf16[8,16,192,512]{3,2,1,0:T(8,128)(2,1)}, u32[]{:S(2)}, u32[]{:S(2)}) %all-to-all-start.3) | async-done | bytes 25165856 | tf_op jit(solution)/shard_map/all_to_all | solution.py:10
  729.0 21.0 %copy.21 = bf16[8,16,192,512]{3,2,0,1:T(8,128)(2,1)} copy(bf16[8,16,192,512]{3,2,1,0:T(8,128)(2,1)} %all-to-all-done.3) | data formatting | bytes 50331648 | tf_op jit(solution)/shard_map/all_to_all | solution.py:10
  750.0 305.7 %while.21 = (s32[]{:T(128)}, f32[16,4,512]{2,1,0:T(4,128)S(1)}, s32[16,1024]{1,0:T(8,128)S(1)}, bf16[24576,512]{1,0:T(8,128)(2,1)}, bf16[256,128]{1,0:T(8,128)(2...) while((s32[]{:T(128)}, f32[16,4,512]{2,1,0:T(4,128)S(1)}, ...), condition=%wide.region_8.9_spmd, body=%wide.region_6.8_spmd.sunk | while | flops 271322112 | bytes 14893685 | solution.py:116
  750.0 15.4 %gather_fusion = bf16[1024,512]{1,0:T(8,128)(2,1)S(1)} fusion(bf16[24576,512]{1,0:T(8,128)(2,1)} %get-tuple-element.293, s32[1024]{0:T(1024)S(1)} %broadcast_clamp_fusion.3), kind=kCustom, calls=%fused_computation.clone.1 | custom fusion | bytes 2101248 | tf_op jit(solution)/shard_map/while/body/eval_jaxpr/gather | solution.py:104
  769.2 15.4 %gather_fusion = bf16[1024,512]{1,0:T(8,128)(2,1)S(1)} fusion(bf16[24576,512]{1,0:T(8,128)(2,1)} %get-tuple-element.293, s32[1024]{0:T(1024)S(1)} %broadcast_clamp_fusion.3), kind=kCustom, calls=%fused_computation.clone.1 | custom fusion | bytes 2101248 | tf_op jit(solution)/shard_map/while/body/eval_jaxpr/gather | solution.py:104
  788.2 15.4 %gather_fusion = bf16[1024,512]{1,0:T(8,128)(2,1)S(1)} fusion(bf16[24576,512]{1,0:T(8,128)(2,1)} %get-tuple-element.293, s32[1024]{0:T(1024)S(1)} %broadcast_clamp_fusion.3), kind=kCustom, calls=%fused_computation.clone.1 | custom fusion | bytes 2101248 | tf_op jit(solution)/shard_map/while/body/eval_jaxpr/gather | solution.py:104
  807.4 15.4 %gather_fusion = bf16[1024,512]{1,0:T(8,128)(2,1)S(1)} fusion(bf16[24576,512]{1,0:T(8,128)(2,1)} %get-tuple-element.293, s32[1024]{0:T(1024)S(1)} %broadcast_clamp_fusion.3), kind=kCustom, calls=%fused_computation.clone.1 | custom fusion | bytes 2101248 | tf_op jit(solution)/shard_map/while/body/eval_jaxpr/gather | solution.py:104
  826.5 15.4 %gather_fusion = bf16[1024,512]{1,0:T(8,128)(2,1)S(1)} fusion(bf16[24576,512]{1,0:T(8,128)(2,1)} %get-tuple-element.293, s32[1024]{0:T(1024)S(1)} %broadcast_clamp_fusion.3), kind=kCustom, calls=%fused_computation.clone.1 | custom fusion | bytes 2101248 | tf_op jit(solution)/shard_map/while/body/eval_jaxpr/gather | solution.py:104
  845.5 15.4 %gather_fusion = bf16[1024,512]{1,0:T(8,128)(2,1)S(1)} fusion(bf16[24576,512]{1,0:T(8,128)(2,1)} %get-tuple-element.293, s32[1024]{0:T(1024)S(1)} %broadcast_clamp_fusion.3), kind=kCustom, calls=%fused_computation.clone.1 | custom fusion | bytes 2101248 | tf_op jit(solution)/shard_map/while/body/eval_jaxpr/gather | solution.py:104
  864.7 15.4 %gather_fusion = bf16[1024,512]{1,0:T(8,128)(2,1)S(1)} fusion(bf16[24576,512]{1,0:T(8,128)(2,1)} %get-tuple-element.293, s32[1024]{0:T(1024)S(1)} %broadcast_clamp_fusion.3), kind=kCustom, calls=%fused_computation.clone.1 | custom fusion | bytes 2101248 | tf_op jit(solution)/shard_map/while/body/eval_jaxpr/gather | solution.py:104
  883.7 15.4 %gather_fusion = bf16[1024,512]{1,0:T(8,128)(2,1)S(1)} fusion(bf16[24576,512]{1,0:T(8,128)(2,1)} %get-tuple-element.293, s32[1024]{0:T(1024)S(1)} %broadcast_clamp_fusion.3), kind=kCustom, calls=%fused_computation.clone.1 | custom fusion | bytes 2101248 | tf_op jit(solution)/shard_map/while/body/eval_jaxpr/gather | solution.py:104
  902.9 15.4 %gather_fusion = bf16[1024,512]{1,0:T(8,128)(2,1)S(1)} fusion(bf16[24576,512]{1,0:T(8,128)(2,1)} %get-tuple-element.293, s32[1024]{0:T(1024)S(1)} %broadcast_clamp_fusion.3), kind=kCustom, calls=%fused_computation.clone.1 | custom fusion | bytes 2101248 | tf_op jit(solution)/shard_map/while/body/eval_jaxpr/gather | solution.py:104
  922.0 15.4 %gather_fusion = bf16[1024,512]{1,0:T(8,128)(2,1)S(1)} fusion(bf16[24576,512]{1,0:T(8,128)(2,1)} %get-tuple-element.293, s32[1024]{0:T(1024)S(1)} %broadcast_clamp_fusion.3), kind=kCustom, calls=%fused_computation.clone.1 | custom fusion | bytes 2101248 | tf_op jit(solution)/shard_map/while/body/eval_jaxpr/gather | solution.py:104
  941.1 15.4 %gather_fusion = bf16[1024,512]{1,0:T(8,128)(2,1)S(1)} fusion(bf16[24576,512]{1,0:T(8,128)(2,1)} %get-tuple-element.293, s32[1024]{0:T(1024)S(1)} %broadcast_clamp_fusion.3), kind=kCustom, calls=%fused_computation.clone.1 | custom fusion | bytes 2101248 | tf_op jit(solution)/shard_map/while/body/eval_jaxpr/gather | solution.py:104
  960.2 15.4 %gather_fusion = bf16[1024,512]{1,0:T(8,128)(2,1)S(1)} fusion(bf16[24576,512]{1,0:T(8,128)(2,1)} %get-tuple-element.293, s32[1024]{0:T(1024)S(1)} %broadcast_clamp_fusion.3), kind=kCustom, calls=%fused_computation.clone.1 | custom fusion | bytes 2101248 | tf_op jit(solution)/shard_map/while/body/eval_jaxpr/gather | solution.py:104
  979.3 15.4 %gather_fusion = bf16[1024,512]{1,0:T(8,128)(2,1)S(1)} fusion(bf16[24576,512]{1,0:T(8,128)(2,1)} %get-tuple-element.293, s32[1024]{0:T(1024)S(1)} %broadcast_clamp_fusion.3), kind=kCustom, calls=%fused_computation.clone.1 | custom fusion | bytes 2101248 | tf_op jit(solution)/shard_map/while/body/eval_jaxpr/gather | solution.py:104
  998.4 15.4 %gather_fusion = bf16[1024,512]{1,0:T(8,128)(2,1)S(1)} fusion(bf16[24576,512]{1,0:T(8,128)(2,1)} %get-tuple-element.293, s32[1024]{0:T(1024)S(1)} %broadcast_clamp_fusion.3), kind=kCustom, calls=%fused_computation.clone.1 | custom fusion | bytes 2101248 | tf_op jit(solution)/shard_map/while/body/eval_jaxpr/gather | solution.py:104
  1017.5 15.4 %gather_fusion = bf16[1024,512]{1,0:T(8,128)(2,1)S(1)} fusion(bf16[24576,512]{1,0:T(8,128)(2,1)} %get-tuple-element.293, s32[1024]{0:T(1024)S(1)} %broadcast_clamp_fusion.3), kind=kCustom, calls=%fused_computation.clone.1 | custom fusion | bytes 2101248 | tf_op jit(solution)/shard_map/while/body/eval_jaxpr/gather | solution.py:104
  1036.6 15.4 %gather_fusion = bf16[1024,512]{1,0:T(8,128)(2,1)S(1)} fusion(bf16[24576,512]{1,0:T(8,128)(2,1)} %get-tuple-element.293, s32[1024]{0:T(1024)S(1)} %broadcast_clamp_fusion.3), kind=kCustom, calls=%fused_computation.clone.1 | custom fusion | bytes 2101248 | tf_op jit(solution)/shard_map/while/body/eval_jaxpr/gather | solution.py:104
  (341 shorter events, 356.2 us)
Async XLA Ops:
  0.0 390.0 %copy-start = (bf16[256,128]{1,0:T(8,128)(2,1)S(1)}, bf16[256,128]{1,0:T(8,128)(2,1)}, u32[]{:S(2)}) copy-start(bf16[256,128]{1,0:T(8,128)(2,1)} %param.15) | copy-start | bytes 196612
  270.6 30.6 %all-to-all-start = ((s32[16,1,192]{2,1,0:T(1,128)}), s32[16,1,192]{2,1,0:T(1,128)S(1)}, u32[]{:S(2)}, u32[]{:S(2)}) async-start(s32[16,1,192]{2,1,0:T(1,128)} %all_to_all.20), calls=%async_computation | async-start | bytes 32768 | tf_op jit(solution)/shard_map/all_to_all | solution.py:94
  381.8 7.5 copy-start.4
  381.8 7.5 copy-start.5
  381.8 8.2 copy-start.7
  381.8 347.2 %all-to-all-start.3 = ((bf16[8,16,192,512]{3,2,1,0:T(8,128)(2,1)}), bf16[8,16,192,512]{3,2,1,0:T(8,128)(2,1)}, u32[]{:S(2)}, u32[]{:S(2)}) async-start(bf16[8,16,192,512]{3,2,1,0:T(8,128)(2,1)} %stack.3), calls=%async_computation.3 | async-start | bytes 50331648 | tf_op jit(solution)/shard_map/all_to_all | solution.py:10
  390.8 359.2 %copy-start.2 = (bf16[256,128]{1,0:T(8,128)(2,1)S(1)}, bf16[256,128]{1,0:T(8,128)(2,1)}, u32[]{:S(2)}) copy-start(bf16[256,128]{1,0:T(8,128)(2,1)} %param.16) | copy-start | bytes 196612
  390.8 359.2 %copy-start.3 = (bf16[256,128]{1,0:T(8,128)(2,1)S(1)}, bf16[256,128]{1,0:T(8,128)(2,1)}, u32[]{:S(2)}) copy-start(bf16[256,128]{1,0:T(8,128)(2,1)} %param.17) | copy-start | bytes 196612
  390.8 359.2 %copy-start.6 = (f32[128]{0:T(128)S(1)}, f32[128]{0:T(128)}, u32[]{:S(2)}) copy-start(f32[128]{0:T(128)} %param.19) | copy-start | bytes 1540
  1055.7 15.0 %copy-start.1 = (bf16[256,128]{1,0:T(8,128)(2,1)S(1)}, bf16[256,128]{1,0:T(8,128)(2,1)}, u32[]{:S(2)}) copy-start(bf16[256,128]{1,0:T(8,128)(2,1)} %param.15) | copy-start | bytes 196612
